TPU v7x, 32 devices: a whole 2x2x4 slice. The times are simulated.
32 devices in a mesh: gx: 4 (over y, x), gy: 4 (over z), gz: 2 (over core).
Axes of the slice: x: 2, y: 2, z: 4, core: 2. Of those that a mesh axis runs over, the one named last changes fastest.
Arguments:
- seg_rows: bfloat16 [4096, 128, 128], P(('gx', 'gy', 'gz')), may hold values from -6 to 6
- owner_map: int32 [4096, 1], replicated, may hold values from 0 to 31; in each aligned block of 128 rows (0 to 127, 128 to 255, ...) at most 8 rows name the same one
- ghost_pick: int32 [32, 1], P(('gx', 'gy', 'gz')), may hold values from 0 to 127
- slab_cost: int32 [4, 4, 2, 3, 1024], P('gx', 'gy', 'gz'), may hold values from 1 to 24
Outputs:
- forces: bfloat16 [32, 32, 8, 128, 128], P(('gx', 'gy', 'gz'))
- cut_points: float32 [7], replicated
Inputs may be any that keep to these rules, and one draw needn't show every extreme that they name: `owner_map`: among the 128 blocks of one device (aligned runs of 128 rows) no owner is named more than 8 times; some device names some owner exactly 8 times.
All inputs are finite; a program needn't handle non-finite values.
Results may differ from a plain program's by a relative error of at most 0.0034.
Values may be sent and summed in bfloat16 or wider, within the bound.
A program may use at most 128 MiB of HBM per device.

v0:
```python
import math
import jax
import jax.numpy as jnp
from jax import lax
from jax.sharding import PartitionSpec as P

sharpness = 8.0
force_gain = 2.0
radius_eps = 0.001


def padded_2(cells, sides, width):
    for axis, dim in sides:
        count = lax.axis_size(axis)
        head = lax.slice_in_dim(cells, 0, width, axis=dim)
        tail = lax.slice_in_dim(cells, cells.shape[dim] - width, cells.shape[dim], axis=dim)
        cells = jnp.concatenate(
            [
                lax.ppermute(tail, axis, [(i, (i + 1) % count) for i in range(count)]),
                cells,
                lax.ppermute(head, axis, [((i + 1) % count, i) for i in range(count)]),
            ],
            axis=dim,
        )
    return cells


def bisect_cuts(histogram):
    running = jnp.cumsum(histogram, axis=1, dtype=jnp.int32)
    total_cost = running[:, -1]
    below = (2 * running < total_cost[:, None]).astype(jnp.int32)
    position = jnp.sum(below, axis=1, dtype=jnp.int32)
    before = jnp.sum(histogram * below, axis=1, dtype=jnp.int32)
    bins_index = lax.broadcasted_iota(jnp.int32, histogram.shape, 1)
    at_cut = jnp.sum(
        jnp.where(bins_index == position[:, None], histogram, 0), axis=1, dtype=jnp.int32
    )
    remain = (total_cost - 2 * before).astype(jnp.float32)
    return (
        position.astype(jnp.float32) + remain / (2 * at_cut).astype(jnp.float32)
    ) / histogram.shape[1]


def kernel_weights(left_sq, right_sq, inner):
    spread = left_sq + right_sq - 2.0 * inner
    return jnp.exp(-sharpness * spread / (left_sq + right_sq + radius_eps)).astype(jnp.bfloat16)


def pair_forces(slot_rows, ghost_set, ghost_sq):
    rows_f = slot_rows.astype(jnp.float32)
    own_sq = jnp.sum(rows_f * rows_f, axis=-1)
    own_inner = jnp.einsum("sbw,scw->sbc", slot_rows, slot_rows, preferred_element_type=jnp.float32)
    ghost_inner = jnp.einsum(
        "sbw,mw->sbm", slot_rows, ghost_set, preferred_element_type=jnp.float32
    )
    own_kernel = kernel_weights(own_sq[:, :, None], own_sq[:, None, :], own_inner)
    ghost_kernel = kernel_weights(own_sq[:, :, None], ghost_sq[None, None, :], ghost_inner)
    weight_sum = jnp.sum(own_kernel.astype(jnp.float32), axis=-1) + jnp.sum(
        ghost_kernel.astype(jnp.float32), axis=-1
    )
    pulled = jnp.einsum("sbc,scw->sbw", own_kernel, slot_rows, preferred_element_type=jnp.float32)
    pulled = pulled + jnp.einsum(
        "sbm,mw->sbw", ghost_kernel, ghost_set, preferred_element_type=jnp.float32
    )
    return (force_gain * (pulled - weight_sum[..., None] * rows_f)).astype(jnp.bfloat16)


def per_device(seg_rows, owner_map, ghost_pick, slab_cost):
    count_x = lax.axis_size("gx")
    count_y = lax.axis_size("gy")
    count_z = lax.axis_size("gz")
    device_count = count_x * count_y * count_z
    blocks_here, block_rows, width = seg_rows.shape
    capacity = max(2, (2 * blocks_here + device_count - 1) // device_count)
    own_index = lax.axis_index(("gx", "gy", "gz"))
    index_x = lax.axis_index("gx")
    index_y = lax.axis_index("gy")
    local_cost = slab_cost[0, 0, 0]
    bins_count = local_cost.shape[1]
    half_part = index_x // (count_x // 2)
    quarter = half_part * 2 + index_y // (count_y // 2)
    x_term = local_cost[0][None]
    y_term = jnp.where(
        lax.broadcasted_iota(jnp.int32, (2, bins_count), 0) == half_part, local_cost[1][None], 0
    )
    z_term = jnp.where(
        lax.broadcasted_iota(jnp.int32, (4, bins_count), 0) == quarter, local_cost[2][None], 0
    )
    histogram = lax.psum(jnp.concatenate([x_term, y_term, z_term], axis=0), ("gx", "gy", "gz"))
    extent = jnp.array([count_x, count_y, count_y, count_z, count_z, count_z, count_z], jnp.float32)
    cut_points = bisect_cuts(histogram) * extent
    exported = jnp.take(seg_rows, ghost_pick[0], axis=0)
    padded = padded_2(exported[None, None, None], (("gx", 0), ("gy", 1), ("gz", 2)), 1)
    ghost_set = jnp.concatenate(
        [
            padded[0, 1, 1],
            padded[2, 1, 1],
            padded[1, 0, 1],
            padded[1, 2, 1],
            padded[1, 1, 0],
            padded[1, 1, 2],
        ],
        axis=0,
    ).reshape(-1, width)
    ghost_float = ghost_set.astype(jnp.float32)
    ghost_sq = jnp.sum(ghost_float * ghost_float, axis=-1)
    all_owners = owner_map[:, 0].reshape(device_count, blocks_here)
    own_owners = lax.dynamic_index_in_dim(all_owners, own_index, 0, keepdims=False)
    block_order = lax.broadcasted_iota(jnp.int32, (blocks_here,), 0)
    earlier = block_order[:, None] < block_order[None, :]
    same_owner = own_owners[:, None] == own_owners[None, :]
    slot_rank = jnp.sum((same_owner & earlier).astype(jnp.int32), axis=0, dtype=jnp.int32)
    slot_of = own_owners * capacity + slot_rank
    slot_ids = lax.broadcasted_iota(jnp.int32, (device_count * capacity,), 0)
    matches = slot_of[None, :] == slot_ids[:, None]
    source_block = jnp.sum(jnp.where(matches, block_order[None, :], 0), axis=1, dtype=jnp.int32)
    filled = jnp.any(matches, axis=1)
    outgoing = jnp.where(
        filled[:, None, None], jnp.take(seg_rows, source_block, axis=0), jnp.zeros((), jnp.bfloat16)
    )
    outgoing = outgoing.reshape(device_count, capacity, block_rows, width)
    arrivals = jnp.sum((all_owners == own_index).astype(jnp.int32), axis=1, dtype=jnp.int32)
    valid_slot = lax.broadcasted_iota(jnp.int32, (device_count, capacity), 1) < arrivals[:, None]
    received = lax.all_to_all(outgoing, ("gx", "gy", "gz"), split_axis=0, concat_axis=0, tiled=True)
    flat_slots = received.reshape(-1, block_rows, width)
    slot_total = flat_slots.shape[0]
    group_size = math.gcd(slot_total, 16)
    grouped = flat_slots.reshape(slot_total // group_size, group_size, block_rows, width)
    settled = lax.map(lambda piece: pair_forces(piece, ghost_set, ghost_sq), grouped)
    forces = settled.reshape(received.shape)
    forces = jnp.where(valid_slot[:, :, None, None], forces, jnp.zeros((), jnp.bfloat16))
    return (forces[None], cut_points)


def solution(mesh):
    return jax.shard_map(
        per_device,
        mesh=mesh,
        in_specs=(
            P(("gx", "gy", "gz"), None, None),
            P(),
            P(("gx", "gy", "gz"), None),
            P("gx", "gy", "gz", None, None),
        ),
        out_specs=(P(("gx", "gy", "gz"), None, None, None, None), P()),
        check_vma=False,
    )
```

profile of v0, /device:TPU:0, one launch (start us, length us, event | category | flops | bytes accessed | tf_op | source)
XLA Modules:
  0.0 430.7 jit_solution(12656038109581809656)
XLA Ops:
  2.6 10.8 %gather_fusion = bf16[256,128,128]{2,1,0:T(8,128)(2,1)} fusion(bf16[128,128,128]{2,1,0:T(8,128)(2,1)} %param.7, s32[1024]{0:T(1024)S(1)} %pad_clamp_fusion), kind=kCustom, calls=%fused_computation | custom fusion | bytes 16778240 | tf_op jit(solution)/shard_map/jit(_take)/gather | solution.py:119
  13.4 7.4 %select_select_fusion = bf16[32,8,128,128]{3,2,1,0:T(8,128)(2,1)} fusion(bf16[32,8,128,128]{3,2,1,0:T(8,128)(2,1)} %bitcast.108, pred[32,8]{1,0:T(8,128)(4,1)S(1)} %compare_and_fusion, pred[32,8]{1,0:T(8,128)(4,1)S(1)} %broadcast_in_dim.117), kind=kLoop, calls=%fused_computation.37 | loop fusion | flops 8388608 | bytes 16777728 | tf_op jit(solution)/shard_map/jit(_where)/select_n | solution.py:118
  20.8 7.5 %all-to-all-start = ((bf16[32,8,128,128]{3,2,1,0:T(8,128)(2,1)}), bf16[32,8,128,128]{3,2,1,0:T(8,128)(2,1)}, u32[]{:S(2)}, u32[]{:S(2)}) async-start(bf16[32,8,128,128]{3,2,1,0:T(8,128)(2,1)} %select_select_fusion), calls=%async_computation | async-start | bytes 16777216 | tf_op jit(solution)/shard_map/all_to_all | solution.py:124
  32.8 199.1 %psum.7 = s32[7,1024]{1,0:T(8,128)S(1)} all-reduce(s32[7,1024]{1,0:T(8,128)S(1)} %pad_add_fusion), channel_id=1, replica_groups=mesh['gx'=4,'gy'=4,'gz'=2] {'gx','gy','gz'}, use_global_device_ids=true, to_apply=%region_10.11 | all-reduce | flops 7168 | bytes 57344 | tf_op jit(solution)/shard_map/psum | solution.py:89
  236.1 3.8 collective-permute-start.3
  239.9 2.9 collective-permute-done.2
  245.1 178.2 %while.11 = (s32[]{:T(128)}, bf16[16,16,128,128]{3,2,1,0:T(8,128)(2,1)}, bf16[16,16,128,128]{3,2,1,0:T(8,128)(2,1)}, f32[768]{0:T(1024)S(1)}, bf16[768,128]{1,0:T(8,128)(2,1)S(1)}, /*index=5*/s32[]{:T(128)}) while((s32[]{:T(128)}, bf16[16,16,128,128]{3,2,1,0:T(8,128)(2,1)}, bf16[16,16,128,128]{3,2,1,0:T(8,128)(2,1)}, f32[768]{0:T(1024)S(1)}, ...), condition=%wide.region_9.10_spmd, body=%wide.region_5.9_spmd.sunk | while | flops 958394368 | bytes 13063241 | solution.py:129
  246.5 3.5 convert_reduce_fusion.8
  257.6 3.5 convert_reduce_fusion.8
  268.8 3.5 convert_reduce_fusion.8
  279.9 3.5 convert_reduce_fusion.8
  291.0 3.5 convert_reduce_fusion.8
  302.1 3.5 convert_reduce_fusion.8
  313.3 3.5 convert_reduce_fusion.8
  324.4 3.5 convert_reduce_fusion.8
  335.5 3.5 convert_reduce_fusion.8
  346.6 3.5 convert_reduce_fusion.8
  357.8 3.5 convert_reduce_fusion.8
  368.9 3.5 convert_reduce_fusion.8
  380.0 3.5 convert_reduce_fusion.8
  391.2 3.5 convert_reduce_fusion.8
  402.4 3.5 convert_reduce_fusion.8
  413.5 3.5 convert_reduce_fusion.8
  423.3 7.4 %broadcast_select_fusion = bf16[1,32,8,128,128]{4,3,2,1,0:T(8,128)(2,1)} fusion(bf16[1,32,8,128,128]{4,3,2,1,0:T(8,128)(2,1)} %bitcast.23, pred[32,8]{1,0:T(8,128)(4,1)S(1)} %iota_compare_fusion.3), kind=kLoop, calls=%fused_computation.38 | loop fusion | flops 4194304 | bytes 16777472 | tf_op jit(solution)/shard_map/jit(_where)/select_n | solution.py:131
  (137 shorter events, 134.1 us)
Async XLA Ops:
  20.8 11.8 %copy-start.1 = (s32[1,1,1,3,1024]{4,2,3,1,0:T(1,128)S(1)}, s32[1,1,1,3,1024]{4,2,3,1,0:T(1,128)}, u32[]{:S(2)}) copy-start(s32[1,1,1,3,1024]{4,2,3,1,0:T(1,128)} %param.10) | copy-start | bytes 36868
  20.8 213.9 %copy-start = (s32[4096,1]{0,1:T(1,128)S(1)}, s32[4096,1]{0,1:T(1,128)}, u32[]{:S(2)}) copy-start(s32[4096,1]{0,1:T(1,128)} %param.8) | copy-start | bytes 49156
  20.8 214.6 %copy-start.2 = (f32[7]{0:T(128)S(1)}, f32[7]{0:T(128)}, u32[]{:S(2)}) copy-start(f32[7]{0:T(128)} %constant.111.clone) | copy-start | bytes 88
  20.8 224.3 %all-to-all-start = ((bf16[32,8,128,128]{3,2,1,0:T(8,128)(2,1)}), bf16[32,8,128,128]{3,2,1,0:T(8,128)(2,1)}, u32[]{:S(2)}, u32[]{:S(2)}) async-start(bf16[32,8,128,128]{3,2,1,0:T(8,128)(2,1)} %select_select_fusion), calls=%async_computation | async-start | bytes 16777216 | tf_op jit(solution)/shard_map/all_to_all | solution.py:124
  29.7 206.3 %collective-permute-start = (bf16[1,1,1,1,128,128]{5,4,3,2,1,0:T(8,128)(2,1)S(1)}, bf16[1,1,1,1,128,128]{5,4,3,2,1,0:T(8,128)(2,1)S(1)}, u32[]{:S(2)}, u32[]{:S(2)}) collective-permute-start(bf16[1,1,1,1,128,128]{5,4,3,2,1,0:T(8,128)(2,1)S(1)} %fusion.32), channel_id=1, source_target_pairs={{0,8},{8,16},{16,24},{24,0},{1,9},{9,17},{17,25},{25,1},{2,10},{10... | collective-permute-start | bytes 98312 | tf_op jit(solution)/shard_map/ppermute | solution.py:19
  31.4 204.6 %collective-permute-start.1 = (bf16[1,1,1,1,128,128]{5,4,3,2,1,0:T(8,128)(2,1)S(1)}, bf16[1,1,1,1,128,128]{5,4,3,2,1,0:T(8,128)(2,1)S(1)}, u32[]{:S(2)}, u32[]{:S(2)}) collective-permute-start(bf16[1,1,1,1,128,128]{5,4,3,2,1,0:T(8,128)(2,1)S(1)} %fusion.32), channel_id=1, source_target_pairs={{8,0},{16,8},{24,16},{0,24},{9,1},{17,9},{25,17},{1,25},{10,2},{18... | collective-permute-start | bytes 98312 | tf_op jit(solution)/shard_map/ppermute | solution.py:21
  236.0 6.8 %collective-permute-start.2 = (bf16[3,1,1,1,128,128]{5,4,3,2,1,0:T(8,128)(2,1)S(1)}, bf16[3,1,1,1,128,128]{5,4,3,2,1,0:T(8,128)(2,1)S(1)}, u32[]{:S(2)}, u32[]{:S(2)}) collective-permute-start(bf16[3,1,1,1,128,128]{5,4,3,2,1,0:T(8,128)(2,1)S(1)} %pad_maximum_fusion.1), channel_id=1, source_target_pairs={{0,2},{2,4},{4,6},{6,0},{1,3},{3,5},{5,7},{7,1},{8,10},{10,12},{12... | collective-permute-start | bytes 294920 | tf_op jit(solution)/shard_map/ppermute | solution.py:19
  236.1 6.7 %collective-permute-start.3 = (bf16[3,1,1,1,128,128]{5,4,3,2,1,0:T(8,128)(2,1)S(1)}, bf16[3,1,1,1,128,128]{5,4,3,2,1,0:T(8,128)(2,1)S(1)}, u32[]{:S(2)}, u32[]{:S(2)}) collective-permute-start(bf16[3,1,1,1,128,128]{5,4,3,2,1,0:T(8,128)(2,1)S(1)} %pad_maximum_fusion.1), channel_id=1, source_target_pairs={{2,0},{4,2},{6,4},{0,6},{3,1},{5,3},{7,5},{1,7},{10,8},{12,10},{14... | collective-permute-start | bytes 294920 | tf_op jit(solution)/shard_map/ppermute | solution.py:21
  242.8 1.6 collective-permute-start.4
  242.9 2.0 collective-permute-start.5
where the time goes:
time: 435 us; the launch traced here: 431 us
  blocking collectives  199 us (46%)
  matrix products  155 us (36%)
  other arithmetic  42.7 us (10%)
  starting transfers between devices  14.8 us (3%)
  local copies, waits for them, and re-layouts  12.2 us (3%)
  waiting for transfers between devices  4.39 us (1%)
    psum x1, blocking collectives, per_device(): lax.psum(jnp.concatenate([x_term, y_term, z_term], axis=0), ('gx', 'gy',...  199 us
    dot_general x16, matrix products, pair_forces(): jnp.einsum('sbw,mw->sbm', slot_rows, ghost_set, preferred_element_type=jn...  55.7 us
    dot_general x16, matrix products, pair_forces(): jnp.einsum('sbm,mw->sbw', ghost_kernel, ghost_set, preferred_element_type...  46 us
    dot_general x16, matrix products, pair_forces(): jnp.einsum('sbw,scw->sbc', slot_rows, slot_rows, preferred_element_type=j...  32.2 us
    reduce_sum x16, other arithmetic, pair_forces(): own_sq = jnp.sum(rows_f * rows_f, axis=-1)  22.1 us
    dot_general x16, matrix products, pair_forces(): jnp.einsum('sbc,scw->sbw', own_kernel, slot_rows, preferred_element_type=...  21.6 us
    gather x1, local copies, waits for them, and re-layouts, per_device(): jnp.take(seg_rows, source_block, axis=0)  10.8 us
  transfers between devices with their start and end apart: 7, of which 3 were waited for; matrix products, arithmetic and copies ran while one was open for 1% of the time, Pallas kernels for 0%

commit v1 on v0

--- a/solution.py
+++ b/solution.py
@@ -86,7 +86,10 @@
     z_term = jnp.where(
         lax.broadcasted_iota(jnp.int32, (4, bins_count), 0) == quarter, local_cost[2][None], 0
     )
-    histogram = lax.psum(jnp.concatenate([x_term, y_term, z_term], axis=0), ("gx", "gy", "gz"))
+    histogram = jnp.sum(
+        lax.all_gather(jnp.concatenate([x_term, y_term, z_term], axis=0), ("gx", "gy", "gz")),
+        axis=0,
+    )
     extent = jnp.array([count_x, count_y, count_y, count_z, count_z, count_z, count_z], jnp.float32)
     cut_points = bisect_cuts(histogram) * extent
     exported = jnp.take(seg_rows, ghost_pick[0], axis=0)

time: 435 us -> 450 us (1.034)
  blocking collectives: 199 us -> 214 us
    all_gather x0 -> x1, blocking collectives: none -> 214 us  [per_device(): lax.all_gather(jnp.concatenate([x_term, y_term, z_term], axis=0), ('gx',...]
    psum x1 -> x0, blocking collectives: 199 us -> none  [per_device(): lax.psum(jnp.concatenate([x_term, y_term, z_term], axis=0), ('gx', 'gy',...]
where the time goes in v1:
time: 450 us; the launch traced here: 446 us
  blocking collectives  214 us (48%)
  matrix products  155 us (34%)
  other arithmetic  42.8 us (10%)
  starting transfers between devices  14.8 us (3%)
  local copies, waits for them, and re-layouts  12.2 us (3%)
  waiting for transfers between devices  5.1 us (1%)
    all_gather x1, blocking collectives, per_device(): lax.all_gather(jnp.concatenate([x_term, y_term, z_term], axis=0), ('gx',...  214 us
    dot_general x16, matrix products, pair_forces(): jnp.einsum('sbw,mw->sbm', slot_rows, ghost_set, preferred_element_type=jn...  55.7 us
    dot_general x16, matrix products, pair_forces(): jnp.einsum('sbm,mw->sbw', ghost_kernel, ghost_set, preferred_element_type...  46 us
    dot_general x16, matrix products, pair_forces(): jnp.einsum('sbw,scw->sbc', slot_rows, slot_rows, preferred_element_type=j...  32.2 us
    reduce_sum x16, other arithmetic, pair_forces(): own_sq = jnp.sum(rows_f * rows_f, axis=-1)  22.1 us
    dot_general x16, matrix products, pair_forces(): jnp.einsum('sbc,scw->sbw', own_kernel, slot_rows, preferred_element_type=...  21.6 us
    gather x1, local copies, waits for them, and re-layouts, per_device(): jnp.take(seg_rows, source_block, axis=0)  10.8 us
  transfers between devices with their start and end apart: 7, of which 3 were waited for; matrix products, arithmetic and copies ran while one was open for 1% of the time, Pallas kernels for 0%

profile of v1, /device:TPU:0, one launch (start us, length us, event | category | flops | bytes accessed | tf_op | source)
XLA Modules:
  0.0 446.1 jit_solution(5421681048913256312)
XLA Ops:
  2.6 10.8 %gather_fusion = bf16[256,128,128]{2,1,0:T(8,128)(2,1)} fusion(bf16[128,128,128]{2,1,0:T(8,128)(2,1)} %param.7, s32[1024]{0:T(1024)S(1)} %pad_clamp_fusion), kind=kCustom, calls=%fused_computation | custom fusion | bytes 16778240 | tf_op jit(solution)/shard_map/jit(_take)/gather | solution.py:122
  13.4 7.4 %select_select_fusion = bf16[32,8,128,128]{3,2,1,0:T(8,128)(2,1)} fusion(bf16[32,8,128,128]{3,2,1,0:T(8,128)(2,1)} %bitcast.110, pred[32,8]{1,0:T(8,128)(4,1)S(1)} %compare_and_fusion, pred[32,8]{1,0:T(8,128)(4,1)S(1)} %broadcast_in_dim.117), kind=kLoop, calls=%fused_computation.37 | loop fusion | flops 8388608 | bytes 16777728 | tf_op jit(solution)/shard_map/jit(_where)/select_n | solution.py:121
  20.8 7.5 %all-to-all-start = ((bf16[32,8,128,128]{3,2,1,0:T(8,128)(2,1)}), bf16[32,8,128,128]{3,2,1,0:T(8,128)(2,1)}, u32[]{:S(2)}, u32[]{:S(2)}) async-start(bf16[32,8,128,128]{3,2,1,0:T(8,128)(2,1)} %select_select_fusion), calls=%async_computation | async-start | bytes 16777216 | tf_op jit(solution)/shard_map/all_to_all | solution.py:127
  32.8 213.7 %all-gather.1 = s32[32,7,1024]{2,1,0:T(8,128)S(1)} all-gather(s32[1,7,1024]{2,1,0:T(8,128)S(1)} %add_bitcast_fusion), channel_id=2, replica_groups=mesh['gx'=4,'gy'=4,'gz'=2] {'gx','gy','gz'}, dimensions={0}, use_global_device_ids=true | all-gather | bytes 946176 | tf_op jit(solution)/shard_map/all_gather | solution.py:90
  250.7 3.8 collective-permute-start.3
  254.6 3.6 collective-permute-done.2
  260.5 178.1 %while.11 = (s32[]{:T(128)}, bf16[16,16,128,128]{3,2,1,0:T(8,128)(2,1)}, bf16[16,16,128,128]{3,2,1,0:T(8,128)(2,1)}, f32[768]{0:T(1024)S(1)}, bf16[768,128]{1,0:T(8,128)(2,1)S(1)}, /*index=5*/s32[]{:T(128)}) while((s32[]{:T(128)}, bf16[16,16,128,128]{3,2,1,0:T(8,128)(2,1)}, bf16[16,16,128,128]{3,2,1,0:T(8,128)(2,1)}, f32[768]{0:T(1024)S(1)}, ...), condition=%wide.region_9.10_spmd, body=%wide.region_5.9_spmd.sunk | while | flops 958394368 | bytes 13063241 | solution.py:132
  261.9 3.5 convert_reduce_fusion.8
  273.0 3.5 convert_reduce_fusion.8
  284.1 3.5 convert_reduce_fusion.8
  295.3 3.5 convert_reduce_fusion.8
  306.4 3.5 convert_reduce_fusion.8
  317.5 3.5 convert_reduce_fusion.8
  328.7 3.5 convert_reduce_fusion.8
  339.8 3.5 convert_reduce_fusion.8
  350.9 3.5 convert_reduce_fusion.8
  362.0 3.5 convert_reduce_fusion.8
  373.1 3.5 convert_reduce_fusion.8
  384.3 3.5 convert_reduce_fusion.8
  395.4 3.5 convert_reduce_fusion.8
  406.5 3.5 convert_reduce_fusion.8
  417.8 3.5 convert_reduce_fusion.8
  428.9 3.5 convert_reduce_fusion.8
  438.6 7.4 %broadcast_select_fusion = bf16[1,32,8,128,128]{4,3,2,1,0:T(8,128)(2,1)} fusion(bf16[1,32,8,128,128]{4,3,2,1,0:T(8,128)(2,1)} %bitcast.23, pred[32,8]{1,0:T(8,128)(4,1)S(1)} %iota_compare_fusion.3), kind=kLoop, calls=%fused_computation.38 | loop fusion | flops 4194304 | bytes 16777472 | tf_op jit(solution)/shard_map/jit(_where)/select_n | solution.py:134
  (138 shorter events, 134.2 us)
Async XLA Ops:
  20.8 11.8 %copy-start.1 = (s32[1,1,1,3,1024]{4,2,3,1,0:T(1,128)S(1)}, s32[1,1,1,3,1024]{4,2,3,1,0:T(1,128)}, u32[]{:S(2)}) copy-start(s32[1,1,1,3,1024]{4,2,3,1,0:T(1,128)} %param.10) | copy-start | bytes 36868
  20.8 228.6 %copy-start = (s32[4096,1]{0,1:T(1,128)S(1)}, s32[4096,1]{0,1:T(1,128)}, u32[]{:S(2)}) copy-start(s32[4096,1]{0,1:T(1,128)} %param.8) | copy-start | bytes 49156
  20.8 229.3 %copy-start.2 = (f32[7]{0:T(128)S(1)}, f32[7]{0:T(128)}, u32[]{:S(2)}) copy-start(f32[7]{0:T(128)} %constant.111.clone) | copy-start | bytes 88
  20.8 239.7 %all-to-all-start = ((bf16[32,8,128,128]{3,2,1,0:T(8,128)(2,1)}), bf16[32,8,128,128]{3,2,1,0:T(8,128)(2,1)}, u32[]{:S(2)}, u32[]{:S(2)}) async-start(bf16[32,8,128,128]{3,2,1,0:T(8,128)(2,1)} %select_select_fusion), calls=%async_computation | async-start | bytes 16777216 | tf_op jit(solution)/shard_map/all_to_all | solution.py:127
  29.7 220.9 %collective-permute-start = (bf16[1,1,1,1,128,128]{5,4,3,2,1,0:T(8,128)(2,1)S(1)}, bf16[1,1,1,1,128,128]{5,4,3,2,1,0:T(8,128)(2,1)S(1)}, u32[]{:S(2)}, u32[]{:S(2)}) collective-permute-start(bf16[1,1,1,1,128,128]{5,4,3,2,1,0:T(8,128)(2,1)S(1)} %fusion.32), channel_id=1, source_target_pairs={{0,8},{8,16},{16,24},{24,0},{1,9},{9,17},{17,25},{25,1},{2,10},{10... | collective-permute-start | bytes 98312 | tf_op jit(solution)/shard_map/ppermute | solution.py:19
  31.4 219.3 %collective-permute-start.1 = (bf16[1,1,1,1,128,128]{5,4,3,2,1,0:T(8,128)(2,1)S(1)}, bf16[1,1,1,1,128,128]{5,4,3,2,1,0:T(8,128)(2,1)S(1)}, u32[]{:S(2)}, u32[]{:S(2)}) collective-permute-start(bf16[1,1,1,1,128,128]{5,4,3,2,1,0:T(8,128)(2,1)S(1)} %fusion.32), channel_id=1, source_target_pairs={{8,0},{16,8},{24,16},{0,24},{9,1},{17,9},{25,17},{1,25},{10,2},{18... | collective-permute-start | bytes 98312 | tf_op jit(solution)/shard_map/ppermute | solution.py:21
  250.7 7.5 %collective-permute-start.2 = (bf16[3,1,1,1,128,128]{5,4,3,2,1,0:T(8,128)(2,1)S(1)}, bf16[3,1,1,1,128,128]{5,4,3,2,1,0:T(8,128)(2,1)S(1)}, u32[]{:S(2)}, u32[]{:S(2)}) collective-permute-start(bf16[3,1,1,1,128,128]{5,4,3,2,1,0:T(8,128)(2,1)S(1)} %pad_maximum_fusion.1), channel_id=1, source_target_pairs={{0,2},{2,4},{4,6},{6,0},{1,3},{3,5},{5,7},{7,1},{8,10},{10,12},{12... | collective-permute-start | bytes 294920 | tf_op jit(solution)/shard_map/ppermute | solution.py:19
  250.7 7.5 %collective-permute-start.3 = (bf16[3,1,1,1,128,128]{5,4,3,2,1,0:T(8,128)(2,1)S(1)}, bf16[3,1,1,1,128,128]{5,4,3,2,1,0:T(8,128)(2,1)S(1)}, u32[]{:S(2)}, u32[]{:S(2)}) collective-permute-start(bf16[3,1,1,1,128,128]{5,4,3,2,1,0:T(8,128)(2,1)S(1)} %pad_maximum_fusion.1), channel_id=1, source_target_pairs={{2,0},{4,2},{6,4},{0,6},{3,1},{5,3},{7,5},{1,7},{10,8},{12,10},{14... | collective-permute-start | bytes 294920 | tf_op jit(solution)/shard_map/ppermute | solution.py:21
  258.2 1.6 collective-permute-start.4
  258.3 2.0 collective-permute-start.5
